TPU v7x, 32 devices: a whole 2x2x4 slice. The times are simulated.
32 devices in a mesh: layer: 4 (over z), row: 2 (over core), col: 4 (over y, x).
Axes of the slice: x: 2, y: 2, z: 4, core: 2. Of those that a mesh axis runs over, the one named last changes fastest.
Arguments:
- panels: float32 [4096, 8192], P('row', ('layer', 'col')), may hold values from -0.0625 to 0.0625
- eigvecs: float32 [8192, 2048], P(('layer', 'row'), 'col'), may hold values from -6 to 6
Outputs:
- result: float32 [4096, 2048], P('row', 'col')
All inputs are finite; a program needn't handle non-finite values.
Results may differ from a plain program's by a relative error of at most 0.0001.
Values sent between devices are 32-bit elements; how exact they have to be, the bound alone decides.
No kernel may reach another device: no remote copies, remote signals or barrier semaphores. Data moves between devices by JAX's collectives and lax.ppermute only.
A program may use at most 64 MiB of HBM per device.

v0:
```python
import jax
import jax.numpy as jnp
from jax import lax
from jax.sharding import PartitionSpec as P


def local(panels, eigvecs):
    layer_vecs = lax.all_gather(eigvecs, "row", axis=0, tiled=True)
    partial_sum = jnp.dot(
        lax.all_gather(panels, "col", axis=1, tiled=True),
        layer_vecs,
        preferred_element_type=jnp.float32,
        precision=lax.Precision.HIGHEST,
    )
    result = lax.psum(partial_sum, "layer")
    return result


def solution(mesh):
    in_specs = (P("row", ("layer", "col")), P(("layer", "row"), "col"))
    out_specs = P("row", "col")
    return jax.shard_map(local, mesh=mesh, in_specs=in_specs, out_specs=out_specs, check_vma=False)
```

profile of v0, /device:TPU:0, one launch (start us, length us, event | category | flops | bytes accessed | tf_op | source)
XLA Modules:
  0.0 383.9 jit_solution(4425001586556484213)
XLA Ops:
  6.5 0.0 all-gather.5.cloned.1.call-start
  6.5 0.7 all-gather.5.cloned.1.call-update
  7.3 0.0 all-gather.3.cloned.1.call-start
  7.3 0.7 all-gather.3.cloned.1.call-update
  8.0 0.0 all-reduce.2.cloned.1.call-start
  8.1 17.2 %all-gather.5.cloned.1.call-done = f32[2048,512]{1,0:T(8,128)} async-done(((f32[1024,512]{1,0:T(8,128)}), f32[2048,512]{1,0:T(8,128)}) %all-gather.5.cloned.1.call-update) | async-done | bytes 4194320 | tf_op jit(solution)/shard_map/all_gather | solution.py:8
  25.3 160.3 %all-gather.3.cloned.1.call-done = f32[2048,2048]{1,0:T(8,128)} async-done(((f32[2048,512]{1,0:T(8,128)}), f32[2048,2048]{1,0:T(8,128)}) %all-gather.3.cloned.1.call-update) | async-done | bytes 16777232 | tf_op jit(solution)/shard_map/all_gather | solution.py:10
  185.6 31.9 %fusion = f32[2048,512]{1,0:T(8,128)} fusion(f32[2048,2048]{1,0:T(8,128)} %all-gather.3.cloned.1.call-done, f32[2048,512]{1,0:T(8,128)} %all-gather.5.cloned.1.call-done), kind=kOutput, calls=%fused_computation | convolution fusion | flops 25769803776 | bytes 25165824 | tf_op jit(solution)/shard_map/dot_general | solution.py:9
  217.6 0.0 all-reduce.2.cloned.1.call-update
  217.6 155.1 %all-reduce.2.cloned.1.call-done = f32[2048,512]{1,0:T(8,128)} async-done(((f32[2048,512]{1,0:T(8,128)}), f32[2048,512]{1,0:T(8,128)}) %all-reduce.2.cloned.1.call-update) | async-done | bytes 4194320 | tf_op jit(solution)/shard_map/psum | solution.py:15
  372.7 4.6 %copy.4 = f32[2048,512]{1,0:T(8,128)} copy(f32[2048,512]{1,0:T(8,128)} %all-reduce.2.cloned.1.call-done) | data formatting | bytes 8388608
Async XLA Ops:
  6.5 18.8 %all-gather.5.cloned.1.call-start = ((), (), s32[]{:S(2)}) async-start(), calls=%async_computation.1 | async-start | bytes 6291456 | tf_op jit(solution)/shard_map/all_gather | solution.py:8
  7.3 178.4 %all-gather.3.cloned.1.call-start = ((), (), s32[]{:S(2)}) async-start(), calls=%async_computation | async-start | bytes 20971520 | tf_op jit(solution)/shard_map/all_gather | solution.py:10
  8.0 364.7 %all-reduce.2.cloned.1.call-start = ((), (), s32[]{:S(2)}) async-start(), calls=%async_computation.2 | async-start | bytes 8388608 | tf_op jit(solution)/shard_map/psum | solution.py:15
Sparse Core Ops, SparseCore 0:
  8.9 16.3 all-gather.4
  27.1 158.4 all-gather.2
  217.7 154.9 all-reduce.1
where the time goes:
time: 384 us
  waiting for transfers between devices  334 us (87%)
  matrix products  31.9 us (8%)
  between operations  13.1 us (3%)
  local copies, waits for them, and re-layouts  4.64 us (1%)
    all_gather x1, waiting for transfers between devices, local(): lax.all_gather(panels, 'col', axis=1, tiled=True)  160 us
    psum x1, waiting for transfers between devices, local(): result = lax.psum(partial_sum, 'layer')  155 us
    dot_general x1, matrix products, local(): jnp.dot(lax.all_gather(panels, 'col', axis=1, tiled=True), layer_vecs, pr...  31.9 us
    all_gather x1, waiting for transfers between devices, local(): layer_vecs = lax.all_gather(eigvecs, 'row', axis=0, tiled=True)  17.2 us
  transfers between devices with their start and end apart: 3, of which 3 were waited for; matrix products, arithmetic and copies ran while one was open for 0% of the time, Pallas kernels for 0%

commit v1 on v0

--- a/solution.py
+++ b/solution.py
@@ -12,7 +12,7 @@
         preferred_element_type=jnp.float32,
         precision=lax.Precision.HIGHEST,
     )
-    result = lax.psum(partial_sum, "layer")
+    result = jnp.sum(lax.all_gather(partial_sum, "layer"), axis=0)
     return result
 
 

time: 384 us -> 522 us (1.36)
  waiting for transfers between devices: 334 us -> 466 us
  other arithmetic: 0 us -> 10.4 us
    all_gather x0 -> x1, waiting for transfers between devices: none -> 287 us  [local(): result = jnp.sum(lax.all_gather(partial_sum, 'layer'), axis=0)]
    psum x1 -> x0, waiting for transfers between devices: 155 us -> none  [local(): result = lax.psum(partial_sum, 'layer')]
    reduce_sum x0 -> x1, other arithmetic: none -> 10.4 us  [local(): result = jnp.sum(lax.all_gather(partial_sum, 'layer'), axis=0)]
where the time goes in v1:
time: 522 us; the launch traced here: 521 us
  waiting for transfers between devices  466 us (89%)
  matrix products  31.9 us (6%)
  between operations  13.1 us (3%)
  other arithmetic  10.4 us (2%)
    all_gather x1, waiting for transfers between devices, local(): result = jnp.sum(lax.all_gather(partial_sum, 'layer'), axis=0)  287 us
    all_gather x1, waiting for transfers between devices, local(): lax.all_gather(panels, 'col', axis=1, tiled=True)  160 us
    dot_general x1, matrix products, local(): jnp.dot(lax.all_gather(panels, 'col', axis=1, tiled=True), layer_vecs, pr...  31.9 us
    all_gather x1, waiting for transfers between devices, local(): layer_vecs = lax.all_gather(eigvecs, 'row', axis=0, tiled=True)  17.2 us
  transfers between devices with their start and end apart: 3, of which 3 were waited for; matrix products, arithmetic and copies ran while one was open for 0% of the time, Pallas kernels for 0%

profile of v1, /device:TPU:0, one launch (start us, length us, event | category | flops | bytes accessed | tf_op | source)
XLA Modules:
  0.0 521.4 jit_solution(11673238801513990992)
XLA Ops:
  6.5 0.0 all-gather.7.cloned.1.call-start
  6.5 0.7 all-gather.7.cloned.1.call-update
  7.3 0.0 all-gather.5.cloned.1.call-start
  7.3 0.7 all-gather.5.cloned.1.call-update
  8.0 0.0 all-gather.9.cloned.1.call-start
  8.1 17.2 %all-gather.7.cloned.1.call-done = f32[2048,512]{1,0:T(8,128)} async-done(((f32[1024,512]{1,0:T(8,128)}), f32[2048,512]{1,0:T(8,128)}) %all-gather.7.cloned.1.call-update) | async-done | bytes 4194320 | tf_op jit(solution)/shard_map/all_gather | solution.py:8
  25.3 160.3 %all-gather.5.cloned.1.call-done = f32[2048,2048]{1,0:T(8,128)} async-done(((f32[2048,512]{1,0:T(8,128)}), f32[2048,2048]{1,0:T(8,128)}) %all-gather.5.cloned.1.call-update) | async-done | bytes 16777232 | tf_op jit(solution)/shard_map/all_gather | solution.py:10
  185.6 31.9 %fusion = f32[2048,512]{1,0:T(8,128)} fusion(f32[2048,2048]{1,0:T(8,128)} %all-gather.5.cloned.1.call-done, f32[2048,512]{1,0:T(8,128)} %all-gather.7.cloned.1.call-done), kind=kOutput, calls=%fused_computation | convolution fusion | flops 25769803776 | bytes 25165824 | tf_op jit(solution)/shard_map/dot_general | solution.py:9
  217.6 0.0 all-gather.9.cloned.1.call-update
  217.6 286.9 %all-gather.9.cloned.1.call-done = f32[8192,512]{1,0:T(8,128)} async-done(((f32[2048,512]{1,0:T(8,128)}), f32[8192,512]{1,0:T(8,128)}) %all-gather.9.cloned.1.call-update) | async-done | bytes 16777232 | tf_op jit(solution)/shard_map/all_gather | solution.py:15
  504.5 10.4 %reduce_sum.9 = f32[2048,512]{1,0:T(8,128)} reduce(f32[4,2048,512]{2,1,0:T(8,128)} %bitcast.3, f32[]{:T(128)} %constant.0.clone.1), dimensions={0}, to_apply=%region_0.0 | reduce | flops 3145728 | bytes 20971524 | tf_op jit(solution)/shard_map/reduce_sum | solution.py:15
Async XLA Ops:
  6.5 18.8 %all-gather.7.cloned.1.call-start = ((), (), s32[]{:S(2)}) async-start(), calls=%async_computation.1 | async-start | bytes 6291456 | tf_op jit(solution)/shard_map/all_gather | solution.py:8
  7.3 178.4 %all-gather.5.cloned.1.call-start = ((), (), s32[]{:S(2)}) async-start(), calls=%async_computation | async-start | bytes 20971520 | tf_op jit(solution)/shard_map/all_gather | solution.py:10
  8.0 496.5 %all-gather.9.cloned.1.call-start = ((), (), s32[]{:S(2)}) async-start(), calls=%async_computation.2 | async-start | bytes 20971520 | tf_op jit(solution)/shard_map/all_gather | solution.py:15
Sparse Core Ops, SparseCore 0:
  8.9 16.3 all-gather.6
  27.1 158.4 all-gather.4
  217.7 286.7 all-gather.8
